TPU v7x, 32 devices: a whole 2x2x4 slice. The times are simulated.
32 devices in a mesh: epoch: 8 (over z, y), blend: 4 (over x, core).
Axes of the slice: x: 2, y: 2, z: 4, core: 2. Of those that a mesh axis runs over, the one named last changes fastest.
Arguments:
- models: float32 [4, 16, 6, 4096], P('blend', 'epoch'), may hold values from -6 to 6
- observed: bfloat16 [8, 64, 4096], P('epoch', 'blend'), may hold values from -6 to 6
- weights: float32 [8, 64], P('epoch', 'blend'), may hold values from 0.5 to 2
- coverage: int32 [8, 64], P('epoch', 'blend'), may hold values from 0 to 1, as said below
- offsets: int32 [8, 64, 2], P('epoch', 'blend'), may hold values from 0 to 63
- counts: int32 [4, 16], P('blend', 'epoch'), may hold values from 1 to 8, as said below
- psf_y: bfloat16 [8, 4096], P('epoch'), may hold values from -0.75 to 0.75
- resample_y: bfloat16 [8, 4096], P('epoch'), may hold values from -0.75 to 0.75
- psf_x: bfloat16 [8, 4096], P('epoch'), may hold values from -0.75 to 0.75
- resample_x: bfloat16 [8, 4096], P('epoch'), may hold values from -0.75 to 0.75
Outputs:
- updated: float32 [4, 16, 6, 4096], P('blend', 'epoch')
Inputs may be any that keep to these rules, and one draw needn't show every extreme that they name: `coverage`: every blend is seen by one epoch or more. counts of blend b is the sum of coverage over all epochs for b.
All inputs are finite; a program needn't handle non-finite values.
Results may differ from a plain program's by a relative error of at most 0.0017.
Values may be sent and summed in bfloat16 or wider, within the bound.
A program may use at most 128 MiB of HBM per device.

v0:
```python
import jax
import jax.numpy as jnp
from jax import lax
from jax.sharding import PartitionSpec as P

CUT = 64
BANDS = 6
PIX2 = 4096


step_size = 0.5


def roll_forward(image, down, across):
    side = image.shape[0]
    doubled = jnp.concatenate([image, image], axis=0)
    rows = lax.dynamic_slice_in_dim(doubled, down, side, 0)
    doubled = jnp.concatenate([rows, rows], axis=1)
    return lax.dynamic_slice_in_dim(doubled, across, side, 1)


def one_epoch(model_low, observed, scale, offsets, left, right, band):
    side = left.shape[0]
    count = observed.shape[0]
    chosen = lax.dynamic_index_in_dim(model_low, band, 1, keepdims=False)
    shifted = jax.vmap(roll_forward)(chosen, offsets[:, 0], offsets[:, 1])
    blurred = jnp.einsum("ij,bjk->bik", left, shifted, preferred_element_type=jnp.float32).astype(
        jnp.bfloat16
    )
    predicted = jnp.einsum("bik,lk->bil", blurred, right, preferred_element_type=jnp.float32)
    target = observed.reshape(count, side, side).astype(jnp.float32)
    misfit = (scale[:, None, None] * (predicted - target)).astype(jnp.bfloat16)
    back = jnp.einsum("ji,bjk->bik", left, misfit, preferred_element_type=jnp.float32).astype(
        jnp.bfloat16
    )
    term = jnp.einsum("bik,kl->bil", back, right, preferred_element_type=jnp.float32)
    return jax.vmap(roll_forward)(term, side - offsets[:, 0], side - offsets[:, 1])


def on_device(
    models, observed, weights, coverage, offsets, counts, psf_y, resample_y, psf_x, resample_x
):
    ep_dev = observed.shape[0]
    group_size = lax.axis_size("epoch")
    all_epochs = ep_dev * group_size
    anchor = lax.axis_index("epoch") * ep_dev
    lefts = jnp.einsum(
        "eij,ejk->eik",
        psf_y.reshape(ep_dev, CUT, CUT),
        resample_y.reshape(ep_dev, CUT, CUT),
        preferred_element_type=jnp.float32,
    ).astype(jnp.bfloat16)
    rights = jnp.einsum(
        "eij,ejk->eik",
        psf_x.reshape(ep_dev, CUT, CUT),
        resample_x.reshape(ep_dev, CUT, CUT),
        preferred_element_type=jnp.float32,
    ).astype(jnp.bfloat16)
    scale = weights * coverage.astype(jnp.float32)
    epoch_bands = (anchor + 0) * BANDS // all_epochs
    first_band = anchor * BANDS // all_epochs
    model_low = models.astype(jnp.bfloat16)
    piece = lax.all_gather(model_low, "epoch", axis=1, tiled=True)
    count = piece.shape[1]
    blocks = piece[0].reshape(count, BANDS, CUT, CUT)
    terms = one_epoch(
        blocks, observed[0], scale[0], offsets[0], lefts[0], rights[0], epoch_bands
    ).reshape(count, PIX2)
    total = jnp.zeros((count, 2, PIX2), jnp.float32)
    slot = epoch_bands - first_band
    current = lax.dynamic_index_in_dim(total, slot, 1, keepdims=False)
    total = lax.dynamic_update_index_in_dim(total, current + terms, slot, 1)
    received = lax.all_to_all(total, "epoch", split_axis=0, concat_axis=1, tiled=True)
    slot_count = received.shape[1]
    position = jnp.arange(slot_count, dtype=jnp.int32)
    source = position // 2
    band_of = source * ep_dev * BANDS // all_epochs + position % 2
    selector = (band_of[:, None] == jnp.arange(BANDS, dtype=jnp.int32)[None, :]).astype(jnp.float32)
    gradient = jnp.einsum("bkp,kc->bcp", received, selector, precision=lax.Precision.HIGHEST)
    divisor = counts[0].astype(jnp.float32)[:, None, None]
    updated = models[0] - step_size * gradient / divisor
    return updated[None]


def solution(mesh):
    return jax.shard_map(
        on_device,
        mesh=mesh,
        in_specs=(
            P("blend", "epoch", None, None),
            P("epoch", "blend", None),
            P("epoch", "blend"),
            P("epoch", "blend"),
            P("epoch", "blend", None),
            P("blend", "epoch"),
            P("epoch", None),
            P("epoch", None),
            P("epoch", None),
            P("epoch", None),
        ),
        out_specs=P("blend", "epoch", None, None),
        check_vma=False,
    )
```

profile of v0, /device:TPU:0, one launch (start us, length us, event | category | flops | bytes accessed | tf_op | source)
XLA Modules:
  0.0 66.9 jit_solution(17146201242047359278)
XLA Ops:
  0.0 1.0 %convert_element_type.47 = bf16[1,2,6,4096]{3,1,2,0:T(2,128)(2,1)S(1)} convert(f32[1,2,6,4096]{3,1,2,0:T(2,128)} %param.10) | non-fusion elementwise | flops 49152 | bytes 294912 | tf_op jit(solution)/shard_map/convert_element_type | solution.py:62
  1.0 0.1 copy.60
  1.1 34.6 %all_gather.3 = bf16[1,16,6,4096]{3,2,0,1:T(8,128)(2,1)S(1)} all-gather(bf16[1,2,6,4096]{3,2,0,1:T(8,128)(2,1)S(1)} %copy.60), channel_id=1, replica_groups=mesh['epoch'=8,'blend'=4] {'epoch'}, dimensions={1}, use_global_device_ids=true | all-gather | bytes 884736 | tf_op jit(solution)/shard_map/all_gather | solution.py:63
  35.7 0.4 copy.61
  36.1 0.0 copy-start.6
  36.1 1.7 %reshape_squeeze.4 = bf16[16,6,64,64]{3,2,0,1:T(8,128)(2,1)S(1)} reshape(bf16[1,16,6,4096]{3,1,2,0:T(8,128)(2,1)S(1)} %copy.61) | data formatting | bytes 1572864 | tf_op jit(solution)/shard_map/reshape;squeeze | solution.py:65
  37.9 0.2 copy.86
  38.1 0.1 pad_maximum_fusion
  38.2 0.0 copy-start.2
  38.2 0.0 copy-start.3
  38.2 0.0 copy-start.4
  38.2 0.0 copy-start.5
  38.3 0.0 copy-start.1
  38.3 1.4 %gather_fusion = bf16[16,64,64]{2,0,1:T(8,128)(2,1)S(1)} fusion(bf16[16,128,64]{2,0,1:T(8,128)(2,1)S(1)} %pad_maximum_fusion, s32[16]{0:T(128)S(1)} %get-tuple-element.6), kind=kCustom, calls=%fused_computation | custom fusion | bytes 262336 | tf_op jit(solution)/shard_map/vmap()/gather | solution.py:17
  39.6 0.1 pad_maximum_fusion.3
  39.8 0.5 copy.63
  40.4 0.1 reduce.2
  40.4 0.1 reshape.76
  40.5 0.1 reduce.3
  40.5 0.1 reshape.77
  40.6 0.1 reduce
  40.7 0.1 reshape.74
  40.8 0.1 reduce.1
  40.8 0.0 copy-start.7
  40.8 0.0 copy-start.8
  40.9 0.1 reshape.75
  40.9 0.2 reshape.78
  41.2 1.4 %gather_fusion.1 = bf16[16,64,64]{1,0,2:T(8,128)(2,1)S(1)} fusion(bf16[16,64,128]{1,0,2:T(8,128)(2,1)S(1)} %copy.63, s32[16]{0:T(128)S(1)} %get-tuple-element.7), kind=kCustom, calls=%fused_computation.1 | custom fusion | bytes 262336 | tf_op jit(solution)/shard_map/vmap()/gather | solution.py:19
  42.5 0.1 fusion.10
  42.7 0.1 fusion.9
  42.8 0.4 fusion.5
  43.3 0.4 fusion.8
  43.7 0.2 pad_maximum_fusion.1
  43.9 0.5 copy.69
  44.4 1.3 %gather_fusion.2 = f32[16,64,64]{2,0,1:T(8,128)S(1)} fusion(f32[16,128,64]{2,0,1:T(8,128)S(1)} %copy.69, s32[16]{0:T(128)S(1)} %get-tuple-element.8), kind=kCustom, calls=%fused_computation.2 | custom fusion | bytes 524480 | tf_op jit(solution)/shard_map/vmap()/gather | solution.py:17
  45.8 0.2 pad_maximum_fusion.2
  46.0 0.6 copy.70
  46.6 1.3 %gather_fusion.3 = f32[16,64,64]{1,0,2:T(8,128)S(1)} fusion(f32[16,64,128]{1,0,2:T(8,128)S(1)} %copy.70, s32[16]{0:T(128)S(1)} %get-tuple-element.5), kind=kCustom, calls=%fused_computation.3 | custom fusion | bytes 524480 | tf_op jit(solution)/shard_map/vmap()/gather | solution.py:19
  47.9 0.3 copy.71
  48.2 0.0 copy-start.9
  48.2 0.3 broadcast_in_dim.8
  48.5 1.0 %dynamic_update_slice.4.clone = f32[16,2,4096]{2,1,0:T(2,128)} pad(f32[16,1,4096]{2,1,0:T(1,128)S(1)} %broadcast_in_dim.8, f32[]{:T(128)} %constant.85.clone.1), padding=0_0x0_1x0_0 | pad | bytes 786436 | tf_op jit(solution)/shard_map/jit(dynamic_update_index_in_dim)/dynamic_update_slice | solution.py:72
  49.5 5.5 %all-to-all-start = ((f32[16,2,4096]{2,1,0:T(2,128)}), f32[16,2,4096]{2,1,0:T(2,128)S(1)}, u32[]{:S(2)}, u32[]{:S(2)}) async-start(f32[16,2,4096]{2,1,0:T(2,128)} %dynamic_update_slice.4.clone), calls=%async_computation | async-start | bytes 1048576 | tf_op jit(solution)/shard_map/all_to_all | solution.py:73
  55.0 0.0 copy-done.9
  55.0 10.3 %all-to-all-done = f32[16,2,4096]{2,1,0:T(2,128)S(1)} async-done(((f32[16,2,4096]{2,1,0:T(2,128)}), f32[16,2,4096]{2,1,0:T(2,128)S(1)}, u32[]{:S(2)}, u32[]{:S(2)}) %all-to-all-start) | async-done | bytes 524320 | tf_op jit(solution)/shard_map/all_to_all | solution.py:73
  65.3 0.4 all_to_all.16
  65.7 0.4 fusion.3
  66.1 0.8 %copy.74 = f32[1,2,6,4096]{3,1,2,0:T(2,128)} copy(f32[1,2,6,4096]{3,2,1,0:T(8,128)S(1)} %fusion.3) | data formatting | bytes 393216 | tf_op jit(solution)/shard_map/broadcast_in_dim | solution.py:82
  (16 shorter events, 0.1 us)
Async XLA Ops:
  36.1 2.1 %copy-start.6 = (s32[1,16,2]{1,2,0:T(2,128)S(1)}, s32[1,16,2]{1,2,0:T(2,128)}, u32[]{:S(2)}) copy-start(s32[1,16,2]{1,2,0:T(2,128)} %param.14) | copy-start | bytes 388
  38.2 2.1 %copy-start.2 = (bf16[1,4096]{1,0:T(2,128)(2,1)S(1)}, bf16[1,4096]{1,0:T(2,128)(2,1)}, u32[]{:S(2)}) copy-start(bf16[1,4096]{1,0:T(2,128)(2,1)} %param.18) | copy-start | bytes 24580
  38.2 2.3 %copy-start.3 = (bf16[1,4096]{1,0:T(2,128)(2,1)S(1)}, bf16[1,4096]{1,0:T(2,128)(2,1)}, u32[]{:S(2)}) copy-start(bf16[1,4096]{1,0:T(2,128)(2,1)} %param.19) | copy-start | bytes 24580
  38.2 2.4 %copy-start.4 = (bf16[1,4096]{1,0:T(2,128)(2,1)S(1)}, bf16[1,4096]{1,0:T(2,128)(2,1)}, u32[]{:S(2)}) copy-start(bf16[1,4096]{1,0:T(2,128)(2,1)} %param.16) | copy-start | bytes 24580
  38.2 2.5 %copy-start.5 = (bf16[1,4096]{1,0:T(2,128)(2,1)S(1)}, bf16[1,4096]{1,0:T(2,128)(2,1)}, u32[]{:S(2)}) copy-start(bf16[1,4096]{1,0:T(2,128)(2,1)} %param.17) | copy-start | bytes 24580
  38.3 2.7 %copy-start.1 = (bf16[1,16,4096]{2,1,0:T(8,128)(2,1)S(1)}, bf16[1,16,4096]{2,1,0:T(8,128)(2,1)}, u32[]{:S(2)}) copy-start(bf16[1,16,4096]{2,1,0:T(8,128)(2,1)} %param.11) | copy-start | bytes 393220
  40.8 2.0 %copy-start.7 = (f32[1,16]{1,0:T(1,128)S(1)}, f32[1,16]{1,0:T(1,128)}, u32[]{:S(2)}) copy-start(f32[1,16]{1,0:T(1,128)} %param.12) | copy-start | bytes 196
  40.8 1.9 %copy-start.8 = (s32[1,16]{1,0:T(1,128)S(1)}, s32[1,16]{1,0:T(1,128)}, u32[]{:S(2)}) copy-start(s32[1,16]{1,0:T(1,128)} %param.13) | copy-start | bytes 196
  48.2 6.9 %copy-start.9 = (s32[1,2]{1,0:T(1,128)S(1)}, s32[1,2]{1,0:T(1,128)}, u32[]{:S(2)}) copy-start(s32[1,2]{1,0:T(1,128)} %param.15) | copy-start | bytes 28
  49.5 16.2 %copy-start = (f32[1,2,6,4096]{3,1,2,0:T(2,128)S(1)}, f32[1,2,6,4096]{3,1,2,0:T(2,128)}, u32[]{:S(2)}) copy-start(f32[1,2,6,4096]{3,1,2,0:T(2,128)} %param.10) | copy-start | bytes 589828
  49.5 15.8 %all-to-all-start = ((f32[16,2,4096]{2,1,0:T(2,128)}), f32[16,2,4096]{2,1,0:T(2,128)S(1)}, u32[]{:S(2)}, u32[]{:S(2)}) async-start(f32[16,2,4096]{2,1,0:T(2,128)} %dynamic_update_slice.4.clone), calls=%async_computation | async-start | bytes 1048576 | tf_op jit(solution)/shard_map/all_to_all | solution.py:73
where the time goes:
time: 67.1 us; the launch traced here: 66.9 us
  blocking collectives  34.6 us (52%)
  local copies, waits for them, and re-layouts  12.8 us (19%)
  waiting for transfers between devices  10.3 us (15%)
  starting transfers between devices  5.52 us (8%)
  other arithmetic  1.9 us (3%)
  matrix products  1.48 us (2%)
    all_gather x1, blocking collectives, on_device(): piece = lax.all_gather(model_low, 'epoch', axis=1, tiled=True)  34.6 us
    all_to_all x1, waiting for transfers between devices, on_device(): lax.all_to_all(total, 'epoch', split_axis=0, concat_axis=1, tiled=True)  10.3 us
    all_to_all x1, starting transfers between devices, on_device(): lax.all_to_all(total, 'epoch', split_axis=0, concat_axis=1, tiled=True)  5.52 us
    gather x3, local copies, waits for them, and re-layouts, roll_forward(): return lax.dynamic_slice_in_dim(doubled, across, side, 1)  2.97 us
    gather x2, local copies, waits for them, and re-layouts, roll_forward(): rows = lax.dynamic_slice_in_dim(doubled, down, side, 0)  2.71 us
    another operation x1, local copies, waits for them, and re-layouts, on_device(): blocks = piece[0].reshape(count, BANDS, CUT, CUT)  1.72 us
  transfers between devices with their start and end apart: 1, of which 1 were waited for; matrix products, arithmetic and copies ran while one was open for 0% of the time, Pallas kernels for 0%

commit v1 on v0

v1 whole, which is shorter than its diff:
```python
import functools

import jax
import jax.numpy as jnp
from jax import lax
from jax.experimental import pallas as pl
from jax.experimental.pallas import tpu as pltpu
from jax.sharding import PartitionSpec as P

step_size = 0.5
LANES = 128
UNROLL = 8
MESH = pl.DeviceIdType.MESH


def dot(a, b):
    return jnp.dot(a, b, preferred_element_type=jnp.float32)


def dot_nt(a, b):
    return lax.dot_general(a, b, (((1,), (1,)), ((), ())), preferred_element_type=jnp.float32)


def each(count, body):
    if count <= UNROLL:
        for step in range(count):
            body(step)
    else:

        @pl.loop(0, count)
        def _(step):
            body(step)


def kernel(
    n,
    models_ref,
    obs_ref,
    weight_ref,
    cover_ref,
    off_ref,
    count_ref,
    psf_y_ref,
    res_y_ref,
    psf_x_ref,
    res_x_ref,
    out_ref,
    wide_ref,
    stage_ref,
    tmp_ref,
    target_ref,
    flat_ref,
    square_ref,
    l_ref,
    lt_ref,
    q_ref,
    model_in,
    term_out,
    term_in,
    model_send,
    model_recv,
    term_send,
    term_recv,
):
    bands, side = stage_ref.shape[0], stage_ref.shape[1]
    chunks = psf_y_ref.shape[1] // LANES
    me = lax.axis_index("epoch")

    barrier = pltpu.get_barrier_semaphore()

    def greet(k):
        pl.semaphore_signal(
            barrier, inc=1, device_id={"epoch": lax.rem(me + k + 1, n)}, device_id_type=MESH
        )

    each(n - 1, greet)

    def first_half(rows):
        return lax.broadcasted_iota(jnp.int32, (rows, LANES), 1) < side

    def pair(even, odd):
        low = first_half(even.shape[0])
        return (
            jnp.where(low, even, pltpu.roll(odd, side, 1)),
            jnp.where(low, pltpu.roll(even, side, 1), odd),
        )

    for c in range(bands):
        even = pl.ds(c * side, side // 2, stride=2)
        odd = pl.ds(c * side + 1, side // 2, stride=2)
        wide_ref[even, :], wide_ref[odd, :] = pair(models_ref[even, :], models_ref[odd, :])
        stage_ref[c] = wide_ref[c * side : (c + 1) * side, :].astype(jnp.bfloat16)

    pl.semaphore_wait(barrier, n - 1)

    def model_copy(k):
        dest = lax.rem(me + k, n)
        return pltpu.make_async_remote_copy(
            src_ref=stage_ref.at[dest * bands // n],
            dst_ref=model_in.at[k],
            send_sem=model_send.at[k],
            recv_sem=model_recv.at[k],
            device_id={"epoch": dest},
            device_id_type=MESH,
        )

    def term_copy(k):
        return pltpu.make_async_remote_copy(
            src_ref=term_out.at[k],
            dst_ref=term_in.at[me],
            send_sem=term_send.at[k],
            recv_sem=term_recv.at[me],
            device_id={"epoch": lax.rem(me - k + n, n)},
            device_id_type=MESH,
        )

    each(n - 1, lambda i: model_copy(n - 1 - i).start())

    def square(ref):
        for c in range(chunks):
            flat_ref[c : c + 1, :] = ref[:, c * LANES : (c + 1) * LANES].astype(jnp.float32)
        square_ref[pl.ds(0, chunks, stride=2), :] = flat_ref[:, :side]
        square_ref[pl.ds(1, chunks, stride=2), :] = flat_ref[:, side:]
        return square_ref[...].astype(jnp.bfloat16)

    left = dot(square(psf_y_ref), square(res_y_ref)).astype(jnp.bfloat16)
    right = dot(square(psf_x_ref), square(res_x_ref)).astype(jnp.bfloat16)
    right_twice = jnp.concatenate([right, right], axis=0)
    row = lax.broadcasted_iota(jnp.int32, (2 * side, side), 0)
    col = lax.broadcasted_iota(jnp.int32, (2 * side, side), 1)
    turn = lax.rem(row - col + side, side)
    top = row < side
    diagonal = (lax.broadcasted_iota(jnp.int32, (LANES, LANES), 0) < side) == (
        lax.broadcasted_iota(jnp.int32, (LANES, LANES), 1) < side
    )

    def operators(s):
        def picks(axis):
            moved = jnp.where(top, off_ref[axis, 2 * s], off_ref[axis, 2 * s + 1])
            return jnp.where(turn == moved, 1.0, 0.0).astype(jnp.bfloat16)

        down, across = picks(0), picks(1)
        lt_ref[s] = dot_nt(down, left).astype(jnp.bfloat16)
        l_ref[s, :side] = dot_nt(left, down[:side]).astype(jnp.bfloat16)
        l_ref[s, side:] = dot_nt(left, down[side:]).astype(jnp.bfloat16)
        q_ref[s] = jnp.where(diagonal, dot_nt(across, right_twice), 0.0).astype(jnp.bfloat16)

    each(n, operators)

    for c in range(chunks):
        at = c * 2 * n
        tmp_ref[at : at + 2 * n, :] = obs_ref[:, c * LANES : (c + 1) * LANES].astype(jnp.float32)
        o0 = tmp_ref[pl.ds(at, n, stride=2), :]
        o1 = tmp_ref[pl.ds(at + 1, n, stride=2), :]
        p0, p1 = pair(o0, o1)
        target_ref[pl.ds(2 * c, n, stride=side), :] = p0
        target_ref[pl.ds(2 * c + 1, n, stride=side), :] = p1

    low = first_half(side)

    def term_of(s, images):
        both = dot(l_ref[s], images)
        blurred = jnp.where(low, both[:side], both[side:]).astype(jnp.bfloat16)
        predicted = dot(blurred, q_ref[s])
        scale = jnp.where(
            low,
            weight_ref[0, 2 * s] * cover_ref[0, 2 * s].astype(jnp.float32),
            weight_ref[0, 2 * s + 1] * cover_ref[0, 2 * s + 1].astype(jnp.float32),
        )
        target = target_ref[pl.ds(pl.multiple_of(s * side, side), side), :]
        misfit = (scale * (predicted - target)).astype(jnp.bfloat16)
        both = dot(lt_ref[s], misfit)
        back = jnp.where(low, both[:side], both[side:]).astype(jnp.bfloat16)
        return dot_nt(back, q_ref[s]).astype(jnp.bfloat16)

    def answer(i):
        k = i + 1
        model_copy(k).wait_recv()
        term_out[k] = term_of(lax.rem(me - k + n, n), model_in[k])
        term_copy(k).start()

    each(n - 1, answer)
    term_in[me] = term_of(me, stage_ref[me * bands // n])

    def collect(i):
        k = i + 1
        source = lax.rem(me + k, n)
        pltpu.make_async_remote_copy(
            src_ref=term_out.at[k],
            dst_ref=term_in.at[source],
            send_sem=term_send.at[k],
            recv_sem=term_recv.at[source],
            device_id={"epoch": source},
            device_id_type=MESH,
        ).wait_recv()

    each(n - 1, collect)

    def factor(i):
        shared = jnp.full((side // 2, LANES), count_ref[0, i], jnp.int32)
        return step_size / shared.astype(jnp.float32)

    f0, f1 = factor(0), factor(1)
    for c in range(bands):
        total = jnp.zeros((side, LANES), jnp.float32)
        for e in range(n):
            if e * bands // n == c:
                total = total + term_in[e].astype(jnp.float32)
        wide_ref[c * side : (c + 1) * side, :] = total
        even = pl.ds(c * side, side // 2, stride=2)
        odd = pl.ds(c * side + 1, side // 2, stride=2)
        g0, g1 = pair(wide_ref[even, :], wide_ref[odd, :])
        out_ref[even, :] = models_ref[even, :] - f0 * g0
        out_ref[odd, :] = models_ref[odd, :] - f1 * g1

    def drain(i):
        model_copy(i + 1).wait_send()
        term_copy(i + 1).wait_send()

    each(n - 1, drain)


def on_device(
    models, observed, weights, coverage, offsets, counts, psf_y, resample_y, psf_x, resample_x
):
    n = lax.axis_size("epoch")
    _, per, bands, pixels = models.shape
    side = round(pixels**0.5)
    assert per * side == LANES and observed.shape[0] == 1 and observed.shape[1] == per * n
    vmem = pl.BlockSpec(memory_space=pltpu.VMEM)
    smem = pl.BlockSpec(memory_space=pltpu.SMEM)
    half = jnp.bfloat16
    chunks = pixels // LANES
    rows = models[0].reshape(per, bands, chunks, LANES).transpose(1, 2, 0, 3)
    updated = pl.pallas_call(
        functools.partial(kernel, n),
        out_shape=jax.ShapeDtypeStruct((bands * side, LANES), jnp.float32),
        in_specs=[vmem, vmem, smem, smem, smem, smem, vmem, vmem, vmem, vmem],
        out_specs=vmem,
        scratch_shapes=[
            pltpu.VMEM((bands * side, LANES), jnp.float32),
            pltpu.VMEM((bands, side, LANES), half),
            pltpu.VMEM((per * n * chunks, LANES), jnp.float32),
            pltpu.VMEM((n * side, LANES), jnp.float32),
            pltpu.VMEM((chunks, LANES), jnp.float32),
            pltpu.VMEM((side, side), jnp.float32),
            pltpu.VMEM((n, 2 * side, side), half),
            pltpu.VMEM((n, 2 * side, side), half),
            pltpu.VMEM((n, LANES, LANES), half),
            pltpu.VMEM((n, side, LANES), half),
            pltpu.VMEM((n, side, LANES), half),
            pltpu.VMEM((n, side, LANES), half),
            pltpu.SemaphoreType.DMA((n,)),
            pltpu.SemaphoreType.DMA((n,)),
            pltpu.SemaphoreType.DMA((n,)),
            pltpu.SemaphoreType.DMA((n,)),
        ],
        compiler_params=pltpu.CompilerParams(collective_id=0, has_side_effects=True),
    )(
        rows.reshape(bands * side, LANES),
        observed[0],
        weights,
        coverage,
        offsets[0].T,
        counts,
        psf_y,
        resample_y,
        psf_x,
        resample_x,
    )
    updated = updated.reshape(bands, chunks, per, LANES).transpose(2, 0, 1, 3)
    return updated.reshape(models.shape)


def solution(mesh):
    return jax.shard_map(
        on_device,
        mesh=mesh,
        in_specs=(
            P("blend", "epoch", None, None),
            P("epoch", "blend", None),
            P("epoch", "blend"),
            P("epoch", "blend"),
            P("epoch", "blend", None),
            P("blend", "epoch"),
            P("epoch", None),
            P("epoch", None),
            P("epoch", None),
            P("epoch", None),
        ),
        out_specs=P("blend", "epoch", None, None),
        check_vma=False,
    )
```

time: 67.1 us -> 19.4 us (0.29)
  blocking collectives: 34.6 us -> 0 us
  Pallas kernels: 0 us -> 17.6 us
  local copies, waits for them, and re-layouts: 12.8 us -> 1.62 us
  waiting for transfers between devices: 10.3 us -> 0 us
  starting transfers between devices: 5.52 us -> 0 us
  other arithmetic: 1.9 us -> 0 us
  matrix products: 1.48 us -> 0 us
    all_gather x1 -> x0, blocking collectives: 34.6 us -> none  [on_device(): piece = lax.all_gather(model_low, 'epoch', axis=1, tiled=True)]
    pallas_call x0 -> x1, Pallas kernels: none -> 17.6 us  [on_device(): pl.pallas_call(functools.partial(kernel, n), out_shape=jax.ShapeDtypeStru...]
    all_to_all x1 -> x0, waiting for transfers between devices: 10.3 us -> none  [on_device(): lax.all_to_all(total, 'epoch', split_axis=0, concat_axis=1, tiled=True)]
    gather x5 -> x0, local copies, waits for them, and re-layouts: 5.68 us -> none  [the longest x3 2.97 us: roll_forward(): return lax.dynamic_slice_in_dim(doubled, across, side, 1)]
    all_to_all x1 -> x0, starting transfers between devices: 5.52 us -> none  [on_device(): lax.all_to_all(total, 'epoch', split_axis=0, concat_axis=1, tiled=True)]
    another operation x4 -> x0, local copies, waits for them, and re-layouts: 1.97 us -> none  [the longest x1 1.72 us: on_device(): blocks = piece[0].reshape(count, BANDS, CUT, CUT)]
    concatenate x3 -> x0, local copies, waits for them, and re-layouts: 1.61 us -> none  [the longest x2 1.11 us: roll_forward(): doubled = jnp.concatenate([rows, rows], axis=1)]
    unnamed x20 -> x1, local copies, waits for them, and re-layouts: 0.06 us -> 1.62 us
  transfers between devices with their start and end apart: 1 -> 0, of which waited for: 1 -> 0; matrix products, arithmetic and copies ran while one was open for 0% -> 0% of each run, Pallas kernels for 0% -> 0%
where the time goes in v1:
time: 19.4 us; the launch traced here: 19.2 us
  Pallas kernels  17.6 us (91%)
  local copies, waits for them, and re-layouts  1.62 us (8%)
    pallas_call x1, Pallas kernels, on_device(): pl.pallas_call(functools.partial(kernel, n), out_shape=jax.ShapeDtypeStru...  17.6 us
    unnamed x1, local copies, waits for them, and re-layouts  1.62 us

profile of v1, /device:TPU:0, one launch (start us, length us, event | category | flops | bytes accessed | tf_op | source)
XLA Modules:
  0.0 19.2 jit_solution(15656964653593405525)
XLA Ops:
  0.0 17.6 %shard_map.100 = f32[384,128]{1,0:T(8,128)} custom-call(f32[384,128]{1,0:T(8,128)} %bitcast.15, bf16[16,4096]{1,0:T(8,128)(2,1)} %bitcast.16, f32[1,16]{1,0:T(1,128)} %weight_ref.1, s32[1,16]{1,0:T(1,128)} %cover_ref.1, s32[2,16]{1,0:T(2,128)} %bitcast.17, s32[1,2]{1,0:T(1,128)} %count_ref.1, bf16[1,4096]{1,0:T(2,128)(2,1)} %psf_y_ref.1, ...), custom_call_target="tpu_custom_call" | custom-call | tf_op jit(solution)/shard_map/pallas_call | solution.py:235
  17.6 1.6 %copy.14 = f32[1,2,6,4096]{3,1,2,0:T(2,128)} copy(f32[1,2,6,4096]{3,1,2,0:T(2,128)} %bitcast.14) | data formatting | bytes 393216

commit v2 on v1

--- a/solution.py
+++ b/solution.py
@@ -34,6 +34,19 @@
 
 def kernel(
     n,
+    *refs,
+):
+    count = 10
+    held = refs[count + 1 : 2 * count + 1]
+    loads = [
+        pltpu.make_async_copy(refs[i], held[i], refs[2 * count + 1].at[i]) for i in range(count)
+    ]
+    body(n, loads, *held, refs[count], *refs[2 * count + 2 :])
+
+
+def body(
+    n,
+    loads,
     models_ref,
     obs_ref,
     weight_ref,
@@ -74,6 +87,8 @@
         )
 
     each(n - 1, greet)
+    for load in loads:
+        load.start()
 
     def first_half(rows):
         return lax.broadcasted_iota(jnp.int32, (rows, LANES), 1) < side
@@ -85,6 +100,7 @@
             jnp.where(low, pltpu.roll(even, side, 1), odd),
         )
 
+    loads[0].wait()
     for c in range(bands):
         even = pl.ds(c * side, side // 2, stride=2)
         odd = pl.ds(c * side + 1, side // 2, stride=2)
@@ -115,6 +131,9 @@
         )
 
     each(n - 1, lambda i: model_copy(n - 1 - i).start())
+
+    for load in loads[1:]:
+        load.wait()
 
     def square(ref):
         for c in range(chunks):
@@ -227,17 +246,33 @@
     _, per, bands, pixels = models.shape
     side = round(pixels**0.5)
     assert per * side == LANES and observed.shape[0] == 1 and observed.shape[1] == per * n
-    vmem = pl.BlockSpec(memory_space=pltpu.VMEM)
-    smem = pl.BlockSpec(memory_space=pltpu.SMEM)
     half = jnp.bfloat16
     chunks = pixels // LANES
     rows = models[0].reshape(per, bands, chunks, LANES).transpose(1, 2, 0, 3)
+    operands = (
+        rows.reshape(bands * side, LANES),
+        observed[0],
+        weights,
+        coverage,
+        offsets[0].T,
+        counts,
+        psf_y,
+        resample_y,
+        psf_x,
+        resample_x,
+    )
+    scalars = range(2, 6)
     updated = pl.pallas_call(
         functools.partial(kernel, n),
-        out_shape=jax.ShapeDtypeStruct((bands * side, LANES), jnp.float32),
-        in_specs=[vmem, vmem, smem, smem, smem, smem, vmem, vmem, vmem, vmem],
-        out_specs=vmem,
+        out_shape=pltpu.VMEM((bands * side, LANES), jnp.float32),
+        in_specs=[pl.BlockSpec(memory_space=pltpu.HBM)] * len(operands),
+        out_specs=pl.BlockSpec(memory_space=pltpu.VMEM),
         scratch_shapes=[
+            (pltpu.SMEM if i in scalars else pltpu.VMEM)(x.shape, x.dtype)
+            for i, x in enumerate(operands)
+        ]
+        + [
+            pltpu.SemaphoreType.DMA((len(operands),)),
             pltpu.VMEM((bands * side, LANES), jnp.float32),
             pltpu.VMEM((bands, side, LANES), half),
             pltpu.VMEM((per * n * chunks, LANES), jnp.float32),
@@ -255,19 +290,8 @@
             pltpu.SemaphoreType.DMA((n,)),
             pltpu.SemaphoreType.DMA((n,)),
         ],
-        compiler_params=pltpu.CompilerParams(collective_id=0, has_side_effects=True),
-    )(
-        rows.reshape(bands * side, LANES),
-        observed[0],
-        weights,
-        coverage,
-        offsets[0].T,
-        counts,
-        psf_y,
-        resample_y,
-        psf_x,
-        resample_x,
-    )
+        compiler_params=pltpu.CompilerParams(collective_id=0, vmem_limit_bytes=32 * 2**20, has_side_effects=True),
+    )(*[pltpu.with_memory_space_constraint(x, pltpu.HBM) for x in operands])
     updated = updated.reshape(bands, chunks, per, LANES).transpose(2, 0, 1, 3)
     return updated.reshape(models.shape)
 

time: 19.4 us -> 16.8 us (0.87)
  Pallas kernels: 17.6 us -> 16 us
  local copies, waits for them, and re-layouts: 1.62 us -> 0.68 us
    pallas_call x1, Pallas kernels: 17.6 us -> 16 us  [on_device(): pl.pallas_call(functools.partial(kernel, n), out_shape=pltpu.VMEM((bands...]
    unnamed x1, local copies, waits for them, and re-layouts: 1.62 us -> 0.68 us
where the time goes in v2:
time: 16.8 us; the launch traced here: 16.7 us
  Pallas kernels  16 us (95%)
  local copies, waits for them, and re-layouts  0.68 us (4%)
    pallas_call x1, Pallas kernels, on_device(): pl.pallas_call(functools.partial(kernel, n), out_shape=pltpu.VMEM((bands...  16 us
    unnamed x1, local copies, waits for them, and re-layouts  0.68 us

profile of v2, /device:TPU:0, one launch (start us, length us, event | category | flops | bytes accessed | tf_op | source)
XLA Modules:
  0.0 16.7 jit_solution(5148970518791285358)
XLA Ops:
  0.0 16.0 %shard_map.100 = f32[384,128]{1,0:T(8,128)S(1)} custom-call(f32[384,128]{1,0:T(8,128)} %bitcast.15, bf16[16,4096]{1,0:T(8,128)(2,1)} %bitcast.16, f32[1,16]{1,0:T(1,128)} %refs_2_.1, s32[1,16]{1,0:T(1,128)} %refs_3_.1, s32[2,16]{1,0:T(2,128)} %bitcast.17, s32[1,2]{1,0:T(1,128)} %refs_5_.1, bf16[1,4096]{1,0:T(2,128)(2,1)} %refs_6_.1, ...), custom_call_target="tpu_custom_call" | custom-call | tf_op jit(solution)/shard_map/pallas_call | solution.py:265
  16.0 0.7 %copy.14 = f32[1,2,6,4096]{3,1,2,0:T(2,128)} copy(f32[1,2,6,4096]{3,1,2,0:T(2,128)S(1)} %bitcast.14) | data formatting | bytes 393216

commit v3 on v2

v3 whole, which is shorter than its diff:
```python
import functools

import jax
import jax.numpy as jnp
from jax import lax
from jax.experimental import pallas as pl
from jax.experimental.pallas import tpu as pltpu
from jax.sharding import PartitionSpec as P

step_size = 0.5
LANES = 128
UNROLL = 8
GROUP = 7
MESH = pl.DeviceIdType.MESH


def dot(a, b):
    return jnp.dot(a, b, preferred_element_type=jnp.float32)


def dot_nt(a, b):
    return lax.dot_general(a, b, (((1,), (1,)), ((), ())), preferred_element_type=jnp.float32)


def each(count, body):
    if count <= UNROLL:
        for step in range(count):
            body(step)
    else:

        @pl.loop(0, count)
        def _(step):
            body(step)


def kernel(
    n,
    nb,
    *refs,
):
    count = 10
    held = refs[count + 1 : 2 * count + 1]
    loads = [
        pltpu.make_async_copy(refs[i], held[i], refs[2 * count + 1].at[i]) for i in range(count)
    ]
    body(n, nb, loads, *held, refs[count], *refs[2 * count + 2 :])


def body(
    n,
    nb,
    loads,
    models_ref,
    obs_ref,
    weight_ref,
    cover_ref,
    off_ref,
    count_ref,
    psf_y_ref,
    res_y_ref,
    psf_x_ref,
    res_x_ref,
    out_ref,
    wide_ref,
    stage_ref,
    tmp_ref,
    target_ref,
    flat_ref,
    square_ref,
    mats,
    seen_out,
    seen_in,
    term_ref,
    mats_send,
    mats_recv,
    seen_send,
    seen_recv,
    relay_send,
    relay_recv,
):
    bands, side = stage_ref.shape[0], mats.shape[1]
    chunks = psf_y_ref.shape[1] // LANES
    me, mine = lax.axis_index("epoch"), lax.axis_index("blend")
    part = pl.ds(pl.multiple_of(mine * (side // nb), side // nb), side // nb)

    barrier = pltpu.get_barrier_semaphore()

    def greet(k):
        pl.semaphore_signal(
            barrier, inc=1, device_id={"epoch": lax.rem(me + k + 1, n)}, device_id_type=MESH
        )

    def greet_twin(k):
        pl.semaphore_signal(
            barrier, inc=1, device_id={"blend": lax.rem(mine + k + 1, nb)}, device_id_type=MESH
        )

    each(n - 1, greet)
    each(nb - 1, greet_twin)
    for load in loads:
        load.start()

    def first_half(rows):
        return lax.broadcasted_iota(jnp.int32, (rows, LANES), 1) < side

    def pair(even, odd):
        low = first_half(even.shape[0])
        return (
            jnp.where(low, even, pltpu.roll(odd, side, 1)),
            jnp.where(low, pltpu.roll(even, side, 1), odd),
        )

    def square(ref):
        for c in range(chunks):
            flat_ref[c : c + 1, :] = ref[:, c * LANES : (c + 1) * LANES].astype(jnp.float32)
        square_ref[pl.ds(0, chunks, stride=2), :] = flat_ref[:, :side]
        square_ref[pl.ds(1, chunks, stride=2), :] = flat_ref[:, side:]
        return square_ref[...].astype(jnp.bfloat16)

    for load in loads[6:]:
        load.wait()
    left = dot(square(psf_y_ref), square(res_y_ref))
    right = dot(square(psf_x_ref), square(res_x_ref))
    mats[me] = jnp.concatenate([left, right], axis=1).astype(jnp.bfloat16)

    for load in loads[1:6]:
        load.wait()
    for c in range(chunks):
        at = c * 2 * n
        tmp_ref[at : at + 2 * n, :] = obs_ref[:, c * LANES : (c + 1) * LANES].astype(jnp.float32)
        o0 = tmp_ref[pl.ds(at, n, stride=2), :]
        o1 = tmp_ref[pl.ds(at + 1, n, stride=2), :]
        p0, p1 = pair(o0, o1)
        target_ref[pl.ds(2 * c, n, stride=side), :] = p0
        target_ref[pl.ds(2 * c + 1, n, stride=side), :] = p1

    notes = seen_out.shape[1] - side
    line = lax.broadcasted_iota(jnp.int32, (notes, LANES), 0)
    low = first_half(notes)

    def pack(d):
        rows = pl.ds(pl.multiple_of(d * side, side), side)
        seen_out[d, :side] = target_ref[rows, :].astype(jnp.bfloat16)
        scale = jnp.where(
            low,
            weight_ref[0, 2 * d] * cover_ref[0, 2 * d].astype(jnp.float32),
            weight_ref[0, 2 * d + 1] * cover_ref[0, 2 * d + 1].astype(jnp.float32),
        )
        high = scale.astype(jnp.bfloat16).astype(jnp.float32)
        mid = (scale - high).astype(jnp.bfloat16).astype(jnp.float32)
        values = [off_ref[axis, 2 * d + i].astype(jnp.float32) for axis in (0, 1) for i in (0, 1)]
        note = jnp.zeros((notes, LANES), jnp.float32)
        for i, value in enumerate(values + [high, mid, scale - high - mid]):
            note = jnp.where(line == i, value, note)
        seen_out[d, side:] = note.astype(jnp.bfloat16)

    each(n, pack)

    pl.semaphore_wait(barrier, n + nb - 2)

    upper = me < n // 2
    longer = jnp.where(upper, n - 1 - me, me)

    def peer(j):
        first = jnp.where(upper, n - 1 - j, j)
        second = jnp.where(upper, j - longer, n - 1 - (j - longer))
        return jnp.where(j < longer, first, second)

    def mats_copy(dest):
        return pltpu.make_async_remote_copy(
            src_ref=mats.at[me, part],
            dst_ref=mats.at[me, part],
            send_sem=mats_send.at[dest],
            recv_sem=mats_recv.at[me],
            device_id={"epoch": dest},
            device_id_type=MESH,
        )

    def mats_arrival(source):
        return pltpu.make_async_remote_copy(
            src_ref=mats.at[source, part],
            dst_ref=mats.at[source, part],
            send_sem=mats_send.at[source],
            recv_sem=mats_recv.at[source],
            device_id={"epoch": source},
            device_id_type=MESH,
        )

    def seen_copy(dest):
        return pltpu.make_async_remote_copy(
            src_ref=seen_out.at[dest],
            dst_ref=seen_in.at[me],
            send_sem=seen_send.at[dest],
            recv_sem=seen_recv.at[me],
            device_id={"epoch": dest},
            device_id_type=MESH,
        )

    def seen_arrival(source):
        return pltpu.make_async_remote_copy(
            src_ref=seen_out.at[source],
            dst_ref=seen_in.at[source],
            send_sem=seen_send.at[source],
            recv_sem=seen_recv.at[source],
            device_id={"epoch": source},
            device_id_type=MESH,
        )

    def relay_copy(source, k):
        return pltpu.make_async_remote_copy(
            src_ref=mats.at[source, part],
            dst_ref=mats.at[source, part],
            send_sem=relay_send.at[k * n + source],
            recv_sem=relay_recv.at[k * n + source],
            device_id={"blend": lax.rem(mine + k, nb)},
            device_id_type=MESH,
        )

    def relay_arrival(source, k):
        twin = lax.rem(mine - k + nb, nb)
        piece = pl.ds(pl.multiple_of(twin * (side // nb), side // nb), side // nb)
        return pltpu.make_async_remote_copy(
            src_ref=mats.at[source, piece],
            dst_ref=mats.at[source, piece],
            send_sem=relay_send.at[k * n + source],
            recv_sem=relay_recv.at[k * n + source],
            device_id={"blend": twin},
            device_id_type=MESH,
        )

    each(n - 1, lambda j: mats_copy(peer(j)).start())
    each(n - 1, lambda j: seen_copy(peer(j)).start())

    low = first_half(side)
    loads[0].wait()
    for c in range(bands):
        even = pl.ds(c * side, side // 2, stride=2)
        odd = pl.ds(c * side + 1, side // 2, stride=2)
        wide_ref[even, :], wide_ref[odd, :] = pair(models_ref[even, :], models_ref[odd, :])
        both = wide_ref[c * side : (c + 1) * side, :]
        stage_ref[c, :side] = jnp.where(low, both, 0.0).astype(jnp.bfloat16)
        stage_ref[c, side:] = jnp.where(low, 0.0, both).astype(jnp.bfloat16)

    row = lax.broadcasted_iota(jnp.int32, (LANES, LANES), 0)
    col = lax.broadcasted_iota(jnp.int32, (LANES, LANES), 1)
    turn = lax.rem(row - col + LANES, side).astype(jnp.float32)
    top, front = row < side, col < side
    diagonal = top == front

    def terms_of(pairs):
        epochs = [e for e, _ in pairs]
        seen = [ref[at] for _, (ref, at) in pairs]
        notes_of = [x[side:].astype(jnp.float32) for x in seen]
        both = [mats[e] for e in epochs]

        def picks(note, first, lanes):
            moved = jnp.where(top, note[first : first + 1], note[first + 1 : first + 2])
            hit = jnp.logical_and(turn == moved, lanes)
            return jnp.where(hit, 1.0, 0.0).astype(jnp.bfloat16)

        down = [picks(x, 0, front) for x in notes_of]
        left = [dot_nt(m, d).astype(jnp.bfloat16) for m, d in zip(both, down)]
        blurred = [
            dot(x, stage_ref[e * bands // n]).astype(jnp.bfloat16) for x, e in zip(left, epochs)
        ]
        across = [picks(x, 2, jnp.logical_not(front)) for x in notes_of]
        right = [
            jnp.where(diagonal, dot_nt(a, jnp.concatenate([m, m], axis=0)), 0.0).astype(
                jnp.bfloat16
            )
            for a, m in zip(across, both)
        ]
        predicted = [dot(x, r) for x, r in zip(blurred, right)]
        left_t = [dot_nt(d, m).astype(jnp.bfloat16) for m, d in zip(both, down)]
        misfit = [
            ((x[4:5] + x[5:6] + x[6:7]) * (p - o[:side].astype(jnp.float32))).astype(jnp.bfloat16)
            for x, p, o in zip(notes_of, predicted, seen)
        ]
        back = [dot(t, x) for t, x in zip(left_t, misfit)]
        back = [jnp.where(low, x[:side], x[side:]).astype(jnp.bfloat16) for x in back]
        terms = [dot_nt(x, r) for x, r in zip(back, right)]
        for e, term in zip(epochs, terms):
            term_ref[e] = term

    terms_of([(me, (seen_out, me))])

    def relay(j):
        source = peer(n - 2 - j)
        mats_arrival(source).wait_recv()
        for k in range(1, nb):
            relay_copy(source, k).start()

    def absorb(js):
        sources = [peer(n - 2 - j) for j in js]
        for source in sources:
            for k in range(1, nb):
                relay_arrival(source, k).wait_recv()
            seen_arrival(source).wait_recv()
        terms_of([(source, (seen_in, source)) for source in sources])

    each(n - 1, relay)
    if n <= UNROLL:
        for first in range(0, n - 1, GROUP):
            absorb(range(first, min(first + GROUP, n - 1)))
    else:
        each(n - 1, lambda j: absorb([j]))

    def factor(i):
        shared = jnp.full((side // 2, LANES), count_ref[0, i], jnp.int32)
        return step_size / shared.astype(jnp.float32)

    f0, f1 = factor(0), factor(1)
    for c in range(bands):
        total = jnp.zeros((side, LANES), jnp.float32)
        for e in range(n):
            if e * bands // n == c:
                total = total + term_ref[e]
        wide_ref[c * side : (c + 1) * side, :] = total
        even = pl.ds(c * side, side // 2, stride=2)
        odd = pl.ds(c * side + 1, side // 2, stride=2)
        g0, g1 = pair(wide_ref[even, :], wide_ref[odd, :])
        out_ref[even, :] = models_ref[even, :] - f0 * g0
        out_ref[odd, :] = models_ref[odd, :] - f1 * g1

    def drain(j):
        mats_copy(peer(j)).wait_send()
        seen_copy(peer(j)).wait_send()
        for k in range(1, nb):
            relay_copy(peer(j), k).wait_send()

    each(n - 1, drain)


def on_device(
    models, observed, weights, coverage, offsets, counts, psf_y, resample_y, psf_x, resample_x
):
    n, nb = lax.axis_size("epoch"), lax.axis_size("blend")
    _, per, bands, pixels = models.shape
    side = round(pixels**0.5)
    assert per * side == LANES and observed.shape[0] == 1 and observed.shape[1] == per * n
    half = jnp.bfloat16
    chunks = pixels // LANES
    rows = models[0].reshape(per, bands, chunks, LANES).transpose(1, 2, 0, 3)
    operands = (
        rows.reshape(bands * side, LANES),
        observed[0],
        weights,
        coverage,
        offsets[0].T,
        counts,
        psf_y,
        resample_y,
        psf_x,
        resample_x,
    )
    scalars = range(2, 6)
    updated = pl.pallas_call(
        functools.partial(kernel, n, nb),
        out_shape=pltpu.VMEM((bands * side, LANES), jnp.float32),
        in_specs=[pl.BlockSpec(memory_space=pltpu.HBM)] * len(operands),
        out_specs=pl.BlockSpec(memory_space=pltpu.VMEM),
        scratch_shapes=[
            (pltpu.SMEM if i in scalars else pltpu.VMEM)(x.shape, x.dtype)
            for i, x in enumerate(operands)
        ]
        + [
            pltpu.SemaphoreType.DMA((len(operands),)),
            pltpu.VMEM((bands * side, LANES), jnp.float32),
            pltpu.VMEM((bands, LANES, LANES), half),
            pltpu.VMEM((per * n * chunks, LANES), jnp.float32),
            pltpu.VMEM((n * side, LANES), jnp.float32),
            pltpu.VMEM((chunks, LANES), jnp.float32),
            pltpu.VMEM((side, side), jnp.float32),
            pltpu.VMEM((n, side, LANES), half),
            pltpu.VMEM((n, side + 16, LANES), half),
            pltpu.VMEM((n, side + 16, LANES), half),
            pltpu.VMEM((n, side, LANES), jnp.float32),
            pltpu.SemaphoreType.DMA((n,)),
            pltpu.SemaphoreType.DMA((n,)),
            pltpu.SemaphoreType.DMA((n,)),
            pltpu.SemaphoreType.DMA((n,)),
            pltpu.SemaphoreType.DMA((nb * n,)),
            pltpu.SemaphoreType.DMA((nb * n,)),
        ],
        compiler_params=pltpu.CompilerParams(collective_id=0, vmem_limit_bytes=32 * 2**20, has_side_effects=True),
    )(*[pltpu.with_memory_space_constraint(x, pltpu.HBM) for x in operands])
    updated = updated.reshape(bands, chunks, per, LANES).transpose(2, 0, 1, 3)
    return updated.reshape(models.shape)


def solution(mesh):
    return jax.shard_map(
        on_device,
        mesh=mesh,
        in_specs=(
            P("blend", "epoch", None, None),
            P("epoch", "blend", None),
            P("epoch", "blend"),
            P("epoch", "blend"),
            P("epoch", "blend", None),
            P("blend", "epoch"),
            P("epoch", None),
            P("epoch", None),
            P("epoch", None),
            P("epoch", None),
        ),
        out_specs=P("blend", "epoch", None, None),
        check_vma=False,
    )
```

time: 16.8 us -> 15.3 us (0.911)
  Pallas kernels: 16 us -> 14.5 us
    pallas_call x1, Pallas kernels: 16 us -> 14.5 us  [on_device(): pl.pallas_call(functools.partial(kernel, n, nb), out_shape=pltpu.VMEM((ba...]
where the time goes in v3:
time: 15.3 us; the launch traced here: 15.2 us
  Pallas kernels  14.5 us (95%)
  local copies, waits for them, and re-layouts  0.68 us (4%)
    pallas_call x1, Pallas kernels, on_device(): pl.pallas_call(functools.partial(kernel, n, nb), out_shape=pltpu.VMEM((ba...  14.5 us
    unnamed x1, local copies, waits for them, and re-layouts  0.68 us

profile of v3, /device:TPU:0, one launch (start us, length us, event | category | flops | bytes accessed | tf_op | source)
XLA Modules:
  0.0 15.2 jit_solution(15437389758097706416)
XLA Ops:
  0.0 14.5 %shard_map.100 = f32[384,128]{1,0:T(8,128)S(1)} custom-call(f32[384,128]{1,0:T(8,128)} %bitcast.15, bf16[16,4096]{1,0:T(8,128)(2,1)} %bitcast.16, f32[1,16]{1,0:T(1,128)} %refs_2_.1, s32[1,16]{1,0:T(1,128)} %refs_3_.1, s32[2,16]{1,0:T(2,128)} %bitcast.17, s32[1,2]{1,0:T(1,128)} %refs_5_.1, bf16[1,4096]{1,0:T(2,128)(2,1)} %refs_6_.1, ...), custom_call_target="tpu_custom_call" | custom-call | tf_op jit(solution)/shard_map/pallas_call | solution.py:357
  14.5 0.7 %copy.14 = f32[1,2,6,4096]{3,1,2,0:T(2,128)} copy(f32[1,2,6,4096]{3,1,2,0:T(2,128)S(1)} %bitcast.14) | data formatting | bytes 393216
